TPU v7x, 32 devices: a whole 2x2x4 slice. The times are simulated.
32 devices in a mesh: seq: 8 (over z, x), head: 4 (over y, core).
Axes of the slice: x: 2, y: 2, z: 4, core: 2. Of those that a mesh axis runs over, the one named last changes fastest.
Arguments:
- values_in: bfloat16 [4096, 4096], P('seq', 'head'), may hold values from -6 to 6
- gate_in: bfloat16 [4096, 4096], P('seq', 'head'), may hold values from -6 to 6
- key_proj: bfloat16 [4096, 128], P('seq'), may hold values from -0.52734375 to 0.52734375
- query_proj: bfloat16 [4096, 128], P('seq'), may hold values from -6 to 6
- step_size: float32 [4096, 64], P('seq', 'head'), may hold values from 0.5 to 2
- log_decay: float32 [4096, 64], P('seq', 'head'), may hold values from -1.2 to 0
- skip_weight: float32 [64], P('head'), may hold values from 0.5 to 1.5
- norm_gain: float32 [4096], P('head'), may hold values from 0.5 to 1.5
- level_table: float32 [16, 64, 7], P(None, 'head'), may hold values from 0.25 to 2
- level_pick: int32 [4096], P('seq'), may hold values from 0 to 15
- doc_start: int32 [64], P('seq'), may hold values 0 or 1
Outputs:
- layer_out: bfloat16 [4096, 4096], P('seq', 'head')
All inputs are finite; a program needn't handle non-finite values. No bound on the sum of `doc_start` on one device may be relied on, other than what follows from the above.
Results may differ from a plain program's by a relative error of at most 0.012.
Values may be sent and summed in bfloat16 or wider, within the bound.
A program may use at most 64 MiB of HBM per device.

v0:
```python
import math

import jax
import jax.numpy as jnp
from jax import lax
from jax.sharding import PartitionSpec as P

H = 64
HEADDIM = 64
STRETCH = 64


epsilon = 1e-06


def partner(array, axis, distance):
    return lax.ppermute(array, axis, [(i, i ^ 1 << distance) for i in range(lax.axis_size(axis))])


def level_of_pairs(row_count, stretch_len, low_bits):
    blocks = jnp.arange(row_count, dtype=jnp.int32) // stretch_len
    differ = jnp.bitwise_xor(blocks[:, None], blocks[None, :])
    level_index = jnp.zeros((row_count, row_count), jnp.int32)
    for bit_index in range(low_bits):
        level_index = level_index + (differ >= 1 << bit_index).astype(jnp.int32)
    return level_index


def local(
    values_in,
    gate_in,
    key_proj,
    query_proj,
    step_size,
    log_decay,
    skip_weight,
    norm_gain,
    level_table,
    level_pick,
    doc_start,
):
    tok_rows = values_in.shape[0]
    head_count = step_size.shape[1]
    head_width = HEADDIM
    state_width = key_proj.shape[1]
    per_span = doc_start.shape[0]
    low_bits = per_span.bit_length() - 1
    span_total = lax.axis_size("seq")
    span_bits = span_total.bit_length() - 1
    table_rows = level_table.shape[0]
    level_count = level_table.shape[2]
    one_hot = (level_pick[:, None] == jnp.arange(table_rows, dtype=jnp.int32)[None, :]).astype(
        jnp.float32
    )
    level_weight = jnp.dot(
        one_hot,
        level_table.reshape(table_rows, head_count * level_count),
        precision=lax.Precision.HIGHEST,
        preferred_element_type=jnp.float32,
    ).reshape(tok_rows, head_count, level_count)
    log_total = jnp.cumsum(log_decay, axis=0)
    doc_stretch = jnp.cumsum(doc_start)
    doc_count = jnp.broadcast_to(doc_stretch[:, None], (per_span, STRETCH)).reshape(tok_rows)
    scaled_in = (jnp.repeat(step_size, head_width, axis=1) * values_in.astype(jnp.float32)).astype(
        jnp.bfloat16
    )
    end_log = log_total[tok_rows - 1]
    tail_decay = (
        jnp.exp(end_log[None, :] - log_total)
        * (doc_count == doc_count[tok_rows - 1]).astype(jnp.float32)[:, None]
    )
    carried_in = (
        jnp.repeat(tail_decay, head_width, axis=1) * scaled_in.astype(jnp.float32)
    ).astype(jnp.bfloat16)
    end_state = jnp.einsum("sc,sn->cn", carried_in, key_proj, preferred_element_type=jnp.float32)
    span_decay = jnp.exp(end_log) * (doc_count[tok_rows - 1] == 0).astype(jnp.float32)
    own_index = lax.axis_index("seq")
    block_state = end_state.reshape(head_count, head_width, state_width)
    block_decay = span_decay
    lead_decay = jnp.ones_like(span_decay)
    level_list = []
    for bit_index in range(span_bits):
        other_state, other_decay = partner((block_state, block_decay), "seq", bit_index)
        is_upper = own_index >> bit_index & 1 == 1
        level_list.append(jnp.where(is_upper, lead_decay[:, None, None] * other_state, 0.0))
        block_state = jnp.where(
            is_upper,
            block_state + block_decay[:, None, None] * other_state,
            other_state + other_decay[:, None, None] * block_state,
        )
        lead_decay = jnp.where(is_upper, lead_decay * other_decay, lead_decay)
        block_decay = block_decay * other_decay
    remote_state = jnp.stack(level_list, 0).astype(jnp.bfloat16)
    level_index = level_of_pairs(tok_rows, STRETCH, low_bits)
    element_position = jnp.arange(tok_rows, dtype=jnp.int32)
    visible = (element_position[:, None] >= element_position[None, :]) & (
        doc_count[:, None] == doc_count[None, :]
    )
    scores = jnp.einsum("tn,sn->ts", query_proj, key_proj, preferred_element_type=jnp.float32)
    reach_decay = jnp.exp(log_total) * (doc_count == 0).astype(jnp.float32)[:, None]
    group_size = math.gcd(head_count, 4)
    group_count = head_count // group_size

    def head_group(inputs):
        group_log, group_weight, group_scaled, group_remote, group_reach = inputs
        select = jnp.zeros((group_size, tok_rows, tok_rows), jnp.float32)
        for level_id in range(low_bits + 1):
            select = select + jnp.where(
                level_index[None] == level_id,
                jnp.transpose(group_weight[:, :, level_id])[:, :, None],
                0.0,
            )
        log_rows = jnp.transpose(group_log)
        log_gap = jnp.where(visible[None], log_rows[:, :, None] - log_rows[:, None, :], -jnp.inf)
        mixing = (scores[None] * select * jnp.exp(log_gap)).astype(jnp.bfloat16)
        local_part = jnp.einsum(
            "hts,shp->thp",
            mixing,
            group_scaled.reshape(tok_rows, group_size, head_width),
            preferred_element_type=jnp.float32,
        )
        projected = jnp.einsum(
            "tn,bhpn->tbhp", query_proj, group_remote, preferred_element_type=jnp.float32
        )
        remote_weight = group_weight[:, :, 1 + low_bits : 1 + low_bits + span_bits]
        remote_part = group_reach[:, :, None] * jnp.einsum(
            "thb,tbhp->thp", remote_weight, projected, precision=lax.Precision.HIGHEST
        )
        return (local_part + remote_part).reshape(tok_rows, group_size * head_width)

    stacked = (
        log_total.reshape(tok_rows, group_count, group_size).transpose(1, 0, 2),
        level_weight.reshape(tok_rows, group_count, group_size, level_count).transpose(1, 0, 2, 3),
        scaled_in.reshape(tok_rows, group_count, group_size * head_width).transpose(1, 0, 2),
        remote_state.reshape(span_bits, group_count, group_size, head_width, state_width).transpose(
            1, 0, 2, 3, 4
        ),
        reach_decay.reshape(tok_rows, group_count, group_size).transpose(1, 0, 2),
    )
    group_parts = lax.map(head_group, stacked)
    both_parts = group_parts.transpose(1, 0, 2).reshape(tok_rows, head_count * head_width)
    combined = both_parts + jnp.repeat(skip_weight, head_width)[None, :] * values_in.astype(
        jnp.float32
    )
    gated_out = combined * jax.nn.silu(gate_in.astype(jnp.float32))
    square_sum = lax.psum(jnp.sum(gated_out * gated_out, axis=1), "head")
    mean_square = square_sum / (H * HEADDIM)
    return (gated_out * lax.rsqrt(mean_square + epsilon)[:, None] * norm_gain[None, :]).astype(
        jnp.bfloat16
    )


def solution(mesh):
    in_specs = (
        P("seq", "head"),
        P("seq", "head"),
        P("seq", None),
        P("seq", None),
        P("seq", "head"),
        P("seq", "head"),
        P("head"),
        P("head"),
        P(None, "head", None),
        P("seq"),
        P("seq"),
    )
    out_specs = P("seq", "head")
    return jax.shard_map(local, mesh=mesh, in_specs=in_specs, out_specs=out_specs, check_vma=False)
```

profile of v0, /device:TPU:0, one launch (start us, length us, event | category | flops | bytes accessed | tf_op | source)
XLA Modules:
  0.0 107.1 jit_solution(10448586130841259728)
XLA Ops:
  0.0 0.9 reduce-window.18
  3.0 1.1 %reduce-window.19 = f32[16,4,128]{2,0,1:T(8,128)S(1)} reduce-window(f32[16,4,128]{2,0,1:T(8,128)S(1)} %copy_bitcast_fusion, f32[]{:T(128)} %constant.67.clone.1), window={size=1x1x128 pad=0_0x0_0x127_0}, to_apply=%region_0.0 | reduce-window | flops 1040384 | bytes 65540 | tf_op jit(solution)/shard_map/reduce-window
  4.6 1.5 %copy.26 = bf16[512,1024]{0,1:T(8,128)(2,1)S(1)} copy(bf16[512,1024]{1,0:T(8,128)(2,1)} %param.13) | data formatting | bytes 2097152 | tf_op args[0]
  7.6 3.0 %collective-permute-start = (f32[16,64,128]{2,1,0:T(8,128)S(1)}, f32[16,64,128]{2,1,0:T(8,128)S(1)}, u32[]{:S(2)}, u32[]{:S(2)}) collective-permute-start(f32[16,64,128]{2,1,0:T(8,128)S(1)} %bitcast.135), channel_id=1, source_target_pairs={{0,4},{4,0},{8,12},{12,8},{16,20},{20,16},{24,28},{28,24},{1,5},{5... | collective-permute-start | bytes 1572872 | tf_op jit(solution)/shard_map/ppermute | solution.py:17
  11.6 11.1 %collective-permute-done.1 = f32[16]{0:T(128)S(1)} collective-permute-done((f32[16]{0:T(128)S(1)}, f32[16]{0:T(128)S(1)}, u32[]{:S(2)}, u32[]{:S(2)}) %collective-permute-start.1) | collective-permute-done | bytes 96 | tf_op jit(solution)/shard_map/ppermute | solution.py:17
  22.7 1.0 add_select_fusion.1
  23.6 1.8 %collective-permute-start.2 = (f32[16,64,128]{2,1,0:T(8,128)}, f32[16,64,128]{2,1,0:T(8,128)}, u32[]{:S(2)}, u32[]{:S(2)}) collective-permute-start(f32[16,64,128]{2,1,0:T(8,128)} %add_select_fusion.1), channel_id=1, source_target_pairs={{0,8},{4,12},{8,0},{12,4},{16,24},{20,28},{24,16},{28,20},{1,9},{5... | collective-permute-start | bytes 1572872 | tf_op jit(solution)/shard_map/ppermute | solution.py:17
  26.0 11.0 %collective-permute-done.3 = f32[16]{0:T(128)S(1)} collective-permute-done((f32[16]{0:T(128)S(1)}, f32[16]{0:T(128)S(1)}, u32[]{:S(2)}, u32[]{:S(2)}) %collective-permute-start.3) | collective-permute-done | bytes 96 | tf_op jit(solution)/shard_map/ppermute | solution.py:17
  37.0 2.2 %select_convert_fusion.1 = (bf16[16,64,128]{2,1,0:T(8,128)(2,1)S(1)}, f32[16,64,128]{2,1,0:T(8,128)}) fusion(f32[16,64,128]{2,1,0:T(8,128)} %collective-permute-done.2, f32[16]{0:T(128)S(1)} %get-tuple-element.185, pred[]{:T(512)S(6)} %eq.101, f32[16,64,128]{2,1,0:T(8,128)} %add_select_fusion.1, f32[16]{0:T(128)S(1)} %collective-permute-done.3, f32[16]{0:T(128)S(1)} %fusion.47), kind=kLoop, calls=%fused_computation.56 | loop fusion | flops 1048576 | bytes 1835201 | tf_op jit(solution)/shard_map/convert.4
  39.2 2.6 %collective-permute-start.4 = (f32[16,64,128]{2,1,0:T(8,128)}, f32[16,64,128]{2,1,0:T(8,128)}, u32[]{:S(2)}, u32[]{:S(2)}) collective-permute-start(f32[16,64,128]{2,1,0:T(8,128)} %get-tuple-element.199), channel_id=1, source_target_pairs={{0,16},{4,20},{8,24},{12,28},{16,0},{20,4},{24,8},{28,12},{1,17},{... | collective-permute-start | bytes 1572872 | tf_op jit(solution)/shard_map/ppermute | solution.py:17
  43.3 2.3 %copy.31 = bf16[512,1024]{0,1:T(8,128)(2,1)} copy(bf16[512,1024]{1,0:T(8,128)(2,1)} %param.14) | data formatting | bytes 2097152 | tf_op args[1]
  45.7 2.2 %fusion.39 = f32[512,512]{1,0:T(8,128)} fusion(bf16[512,128]{1,0:T(8,128)(2,1)} %param.16, bf16[512,128]{1,0:T(8,128)(2,1)S(1)} %copy-done), kind=kOutput, calls=%fused_computation.82 | convolution fusion | flops 67108864 | bytes 1310720 | tf_op jit(solution)/shard_map/tn,sn->ts/dot_general | solution.py:99
  48.0 15.8 %collective-permute-done.4 = f32[16,64,128]{2,1,0:T(8,128)} collective-permute-done((f32[16,64,128]{2,1,0:T(8,128)}, f32[16,64,128]{2,1,0:T(8,128)}, u32[]{:S(2)}, u32[]{:S(2)}) %collective-permute-start.4) | collective-permute-done | bytes 524320 | tf_op jit(solution)/shard_map/ppermute | solution.py:17
  63.8 1.2 %select_convert_fusion = bf16[16,64,128]{2,1,0:T(8,128)(2,1)S(1)} fusion(f32[16,64,128]{2,1,0:T(8,128)} %collective-permute-done.4, f32[16]{0:T(128)S(1)} %get-tuple-element.184, pred[]{:T(512)S(6)} %eq.103), kind=kLoop, calls=%fused_computation.54 | loop fusion | flops 393216 | bytes 786497 | tf_op jit(solution)/shard_map/convert.3
  65.0 1.0 maximum_bitcast_fusion
  65.9 31.2 %while.12 = (s32[]{:T(128)}, f32[4,512,256]{1,2,0:T(8,128)}, bf16[4,512,256]{1,2,0:T(8,128)(2,1)S(1)}, f32[512,512]{1,0:T(8,128)}, f32[4,512,4,7]{1,2,3,0:T(4,12...) while((s32[]{:T(128)}, f32[4,512,256]{1,2,0:T(8,128)}, ...), condition=%wide.region_4.5_spmd.clone.clone, body=%wide.region_3.4_spmd.clone.clone.sunk | while | flops 252575744 | bytes 11941021 | solution.py:140
  65.9 1.5 %fusion.61 = f32[512,4,64]{0,2,1:T(8,128)S(1)} fusion(f32[512,4,3]{0,1,2:T(4,128)S(1)} %slice.58, bf16[4,3,4,64,128]{4,3,2,1,0:T(8,128)(2,1)} %get-tuple-element.322, s32[]{:T(128)} %get-tuple-element.303, bf16[512,128]{1,0:T(8,128)(2,1)} %get-tuple-element.323), kind=kOutput, calls=%fused_computation.13.clone.1 | convolution fusion | flops 101318656 | bytes 877056 | tf_op jit(solution)/shard_map/while/body/eval_jaxpr/tn,bhpn->tbhp/dot_general | solution.py:122
  68.2 0.9 fusion.60
  69.3 3.5 %fusion.62 = f32[512,4,64]{0,2,1:T(8,128)S(1)} fusion(bf16[512,4,64]{0,2,1:T(8,128)(2,1)S(1)} %bitcast.133, f32[4,512]{1,0:T(4,128)S(1)} %get-tuple-element.281, f32[4,512]{1,0:T(4,128)S(1)} %get-tuple-element.282, f32[4,512]{1,0:T(4,128)S(1)} %get-tuple-element.283, f32[4,512]{1,0:T(4,128)S(1)} %get-tuple-element.284, ...), kind=kOutput, calls=%fused_computation.15.clone.1 | convolution fusion | flops 147062784 | bytes 3719168 | tf_op jit(solution)/shard_map/while/body/eval_jaxpr/hts,shp->thp/dot_general | solution.py:116
  73.7 1.5 %fusion.61 = f32[512,4,64]{0,2,1:T(8,128)S(1)} fusion(f32[512,4,3]{0,1,2:T(4,128)S(1)} %slice.58, bf16[4,3,4,64,128]{4,3,2,1,0:T(8,128)(2,1)} %get-tuple-element.322, s32[]{:T(128)} %get-tuple-element.303, bf16[512,128]{1,0:T(8,128)(2,1)} %get-tuple-element.323), kind=kOutput, calls=%fused_computation.13.clone.1 | convolution fusion | flops 101318656 | bytes 877056 | tf_op jit(solution)/shard_map/while/body/eval_jaxpr/tn,bhpn->tbhp/dot_general | solution.py:122
  75.9 0.9 fusion.60
  77.1 3.5 %fusion.62 = f32[512,4,64]{0,2,1:T(8,128)S(1)} fusion(bf16[512,4,64]{0,2,1:T(8,128)(2,1)S(1)} %bitcast.133, f32[4,512]{1,0:T(4,128)S(1)} %get-tuple-element.281, f32[4,512]{1,0:T(4,128)S(1)} %get-tuple-element.282, f32[4,512]{1,0:T(4,128)S(1)} %get-tuple-element.283, f32[4,512]{1,0:T(4,128)S(1)} %get-tuple-element.284, ...), kind=kOutput, calls=%fused_computation.15.clone.1 | convolution fusion | flops 147062784 | bytes 3719168 | tf_op jit(solution)/shard_map/while/body/eval_jaxpr/hts,shp->thp/dot_general | solution.py:116
  81.5 1.5 %fusion.61 = f32[512,4,64]{0,2,1:T(8,128)S(1)} fusion(f32[512,4,3]{0,1,2:T(4,128)S(1)} %slice.58, bf16[4,3,4,64,128]{4,3,2,1,0:T(8,128)(2,1)} %get-tuple-element.322, s32[]{:T(128)} %get-tuple-element.303, bf16[512,128]{1,0:T(8,128)(2,1)} %get-tuple-element.323), kind=kOutput, calls=%fused_computation.13.clone.1 | convolution fusion | flops 101318656 | bytes 877056 | tf_op jit(solution)/shard_map/while/body/eval_jaxpr/tn,bhpn->tbhp/dot_general | solution.py:122
  83.7 0.9 fusion.60
  84.9 3.5 %fusion.62 = f32[512,4,64]{0,2,1:T(8,128)S(1)} fusion(bf16[512,4,64]{0,2,1:T(8,128)(2,1)S(1)} %bitcast.133, f32[4,512]{1,0:T(4,128)S(1)} %get-tuple-element.281, f32[4,512]{1,0:T(4,128)S(1)} %get-tuple-element.282, f32[4,512]{1,0:T(4,128)S(1)} %get-tuple-element.283, f32[4,512]{1,0:T(4,128)S(1)} %get-tuple-element.284, ...), kind=kOutput, calls=%fused_computation.15.clone.1 | convolution fusion | flops 147062784 | bytes 3719168 | tf_op jit(solution)/shard_map/while/body/eval_jaxpr/hts,shp->thp/dot_general | solution.py:116
  88.4 0.9 constant_dynamic-update-slice_fusion.2
  89.3 1.5 %fusion.61 = f32[512,4,64]{0,2,1:T(8,128)S(1)} fusion(f32[512,4,3]{0,1,2:T(4,128)S(1)} %slice.58, bf16[4,3,4,64,128]{4,3,2,1,0:T(8,128)(2,1)} %get-tuple-element.322, s32[]{:T(128)} %get-tuple-element.303, bf16[512,128]{1,0:T(8,128)(2,1)} %get-tuple-element.323), kind=kOutput, calls=%fused_computation.13.clone.1 | convolution fusion | flops 101318656 | bytes 877056 | tf_op jit(solution)/shard_map/while/body/eval_jaxpr/tn,bhpn->tbhp/dot_general | solution.py:122
  91.5 0.9 fusion.60
  92.7 3.5 %fusion.62 = f32[512,4,64]{0,2,1:T(8,128)S(1)} fusion(bf16[512,4,64]{0,2,1:T(8,128)(2,1)S(1)} %bitcast.133, f32[4,512]{1,0:T(4,128)S(1)} %get-tuple-element.281, f32[4,512]{1,0:T(4,128)S(1)} %get-tuple-element.282, f32[4,512]{1,0:T(4,128)S(1)} %get-tuple-element.283, f32[4,512]{1,0:T(4,128)S(1)} %get-tuple-element.284, ...), kind=kOutput, calls=%fused_computation.15.clone.1 | convolution fusion | flops 147062784 | bytes 3719168 | tf_op jit(solution)/shard_map/while/body/eval_jaxpr/hts,shp->thp/dot_general | solution.py:116
  97.1 2.8 %multiply_reduce_fusion = (f32[512]{0:T(512)S(1)}, f32[512,1024]{0,1:T(8,128)S(1)}) fusion(bf16[512,1024]{0,1:T(8,128)(2,1)} %copy.31, bf16[512,1024]{0,1:T(8,128)(2,1)S(1)} %copy.26, f32[1024]{0:T(1024)S(1)} %mul.165, f32[4,512,256]{1,2,0:T(8,128)} %get-tuple-element.71), kind=kLoop, calls=%fused_computation.51 | loop fusion | flops 5766656 | bytes 6297600 | tf_op jit(solution)/shard_map/reduce_sum | solution.py:146
  99.9 5.7 %psum.7 = f32[512]{0:T(512)S(1)} all-reduce(f32[512]{0:T(512)S(1)} %get-tuple-element.182), channel_id=1, replica_groups=mesh['seq'=8,'head'=4] {'head'}, use_global_device_ids=true, to_apply=%region_6.7 | all-reduce | flops 512 | bytes 4096 | tf_op jit(solution)/shard_map/psum | solution.py:146
  105.8 1.3 %copy.32 = bf16[512,1024]{1,0:T(8,128)(2,1)} copy(bf16[512,1024]{0,1:T(8,128)(2,1)S(1)} %multiply_convert_fusion.6) | data formatting | bytes 2097152 | tf_op jit(solution)/shard_map/convert_element_type | solution.py:148
  (81 shorter events, 13.1 us)
Async XLA Ops:
  0.0 7.2 %copy-start = (bf16[512,128]{1,0:T(8,128)(2,1)S(1)}, bf16[512,128]{1,0:T(8,128)(2,1)}, u32[]{:S(2)}) copy-start(bf16[512,128]{1,0:T(8,128)(2,1)} %param.15) | copy-start | bytes 393220
  0.0 6.8 %copy-start.3 = (f32[512,16]{0,1:T(8,128)S(1)}, f32[512,16]{0,1:T(8,128)}, u32[]{:S(2)}) copy-start(f32[512,16]{0,1:T(8,128)} %param.17) | copy-start | bytes 98308
  6.8 4.6 %copy-start.2 = (f32[16,16,7]{1,0,2:T(8,128)S(1)}, f32[16,16,7]{1,0,2:T(8,128)}, u32[]{:S(2)}) copy-start(f32[16,16,7]{1,0,2:T(8,128)} %param.21) | copy-start | bytes 21508
  7.2 18.3 %copy-start.5 = (s32[512]{0:T(512)S(1)}, s32[512]{0:T(512)}, u32[]{:S(2)}) copy-start(s32[512]{0:T(512)} %param.22) | copy-start | bytes 6148
  7.6 15.0 %collective-permute-start = (f32[16,64,128]{2,1,0:T(8,128)S(1)}, f32[16,64,128]{2,1,0:T(8,128)S(1)}, u32[]{:S(2)}, u32[]{:S(2)}) collective-permute-start(f32[16,64,128]{2,1,0:T(8,128)S(1)} %bitcast.135), channel_id=1, source_target_pairs={{0,4},{4,0},{8,12},{12,8},{16,20},{20,16},{24,28},{28,24},{1,5},{5... | collective-permute-start | bytes 1572872 | tf_op jit(solution)/shard_map/ppermute | solution.py:17
  11.3 11.3 %collective-permute-start.1 = (f32[16]{0:T(128)S(1)}, f32[16]{0:T(128)S(1)}, u32[]{:S(2)}, u32[]{:S(2)}) collective-permute-start(f32[16]{0:T(128)S(1)} %exponential_multiply_fusion.2), channel_id=1, source_target_pairs={{0,4},{4,0},{8,12},{12,8},{16,20},{20,16},{24,28},{28,24},{1,5},{5... | collective-permute-start | bytes 200 | tf_op jit(solution)/shard_map/ppermute | solution.py:17
  23.6 13.3 %collective-permute-start.2 = (f32[16,64,128]{2,1,0:T(8,128)}, f32[16,64,128]{2,1,0:T(8,128)}, u32[]{:S(2)}, u32[]{:S(2)}) collective-permute-start(f32[16,64,128]{2,1,0:T(8,128)} %add_select_fusion.1), channel_id=1, source_target_pairs={{0,8},{4,12},{8,0},{12,4},{16,24},{20,28},{24,16},{28,20},{1,9},{5... | collective-permute-start | bytes 1572872 | tf_op jit(solution)/shard_map/ppermute | solution.py:17
  25.7 11.2 %collective-permute-start.3 = (f32[16]{0:T(128)S(1)}, f32[16]{0:T(128)S(1)}, u32[]{:S(2)}, u32[]{:S(2)}) collective-permute-start(f32[16]{0:T(128)S(1)} %fusion.47), channel_id=1, source_target_pairs={{0,8},{4,12},{8,0},{12,4},{16,24},{20,28},{24,16},{28,20},{1,9},{5... | collective-permute-start | bytes 200 | tf_op jit(solution)/shard_map/ppermute | solution.py:17
  39.2 6.4 %copy-start.6 = (f32[16]{0:T(128)S(1)}, f32[16]{0:T(128)}, u32[]{:S(2)}) copy-start(f32[16]{0:T(128)} %param.19) | copy-start | bytes 196
  39.2 24.6 %collective-permute-start.4 = (f32[16,64,128]{2,1,0:T(8,128)}, f32[16,64,128]{2,1,0:T(8,128)}, u32[]{:S(2)}, u32[]{:S(2)}) collective-permute-start(f32[16,64,128]{2,1,0:T(8,128)} %get-tuple-element.199), channel_id=1, source_target_pairs={{0,16},{4,20},{8,24},{12,28},{16,0},{20,4},{24,8},{28,12},{1,17},{... | collective-permute-start | bytes 1572872 | tf_op jit(solution)/shard_map/ppermute | solution.py:17
  65.9 3.4 %copy-start.1 = (f32[512,512]{1,0:T(8,128)S(1)}, f32[512,512]{1,0:T(8,128)}, u32[]{:S(2)}) copy-start(f32[512,512]{1,0:T(8,128)} %get-tuple-element.318) | copy-start | bytes 3145732 | tf_op jit(solution)/shard_map/while
  73.7 3.4 %copy-start.1 = (f32[512,512]{1,0:T(8,128)S(1)}, f32[512,512]{1,0:T(8,128)}, u32[]{:S(2)}) copy-start(f32[512,512]{1,0:T(8,128)} %get-tuple-element.318) | copy-start | bytes 3145732 | tf_op jit(solution)/shard_map/while
  81.5 3.4 %copy-start.1 = (f32[512,512]{1,0:T(8,128)S(1)}, f32[512,512]{1,0:T(8,128)}, u32[]{:S(2)}) copy-start(f32[512,512]{1,0:T(8,128)} %get-tuple-element.318) | copy-start | bytes 3145732 | tf_op jit(solution)/shard_map/while
  89.3 3.4 %copy-start.1 = (f32[512,512]{1,0:T(8,128)S(1)}, f32[512,512]{1,0:T(8,128)}, u32[]{:S(2)}) copy-start(f32[512,512]{1,0:T(8,128)} %get-tuple-element.318) | copy-start | bytes 3145732 | tf_op jit(solution)/shard_map/while
  97.1 8.5 %copy-start.4 = (f32[1024]{0:T(1024)S(1)}, f32[1024]{0:T(1024)}, u32[]{:S(2)}) copy-start(f32[1024]{0:T(1024)} %param.20) | copy-start | bytes 12292
where the time goes:
time: 108 us; the launch traced here: 107 us
  waiting for transfers between devices  37.9 us (35%)
  matrix products  22.9 us (21%)
  other arithmetic  16.8 us (16%)
  local copies, waits for them, and re-layouts  15.1 us (14%)
  starting transfers between devices  7.77 us (7%)
  blocking collectives  5.66 us (5%)
    ppermute x5, waiting for transfers between devices, partner(): lax.ppermute(array, axis, [(i, i ^ 1 << distance) for i in range(lax.axis...  37.9 us
    dot_general x4, matrix products, head_group(): jnp.einsum('hts,shp->thp', mixing, group_scaled.reshape(tok_rows, group_s...  14.1 us
    ppermute x5, starting transfers between devices, partner(): lax.ppermute(array, axis, [(i, i ^ 1 << distance) for i in range(lax.axis...  7.77 us
    dot_general x4, matrix products, head_group(): jnp.einsum('tn,bhpn->tbhp', query_proj, group_remote, preferred_element_t...  5.92 us
    psum x1, blocking collectives, local(): square_sum = lax.psum(jnp.sum(gated_out * gated_out, axis=1), 'head')  5.66 us
    another operation x7, other arithmetic  5.55 us
    unnamed x16, local copies, waits for them, and re-layouts  4.04 us
    eq x4, other arithmetic, head_group(): level_index[None] == level_id  3.76 us
  transfers between devices with their start and end apart: 5, of which 3 were waited for; matrix products, arithmetic and copies ran while one was open for 6% of the time, Pallas kernels for 0%

commit v1 on v0

v1 whole, which is shorter than its diff:
```python
import functools

import jax
import jax.numpy as jnp
from jax import lax
from jax.experimental import pallas as pl
from jax.experimental.pallas import tpu as pltpu
from jax.sharding import PartitionSpec as P

HEADDIM = 64
STRETCH = 64
CHUNKS = 4

epsilon = 1e-06
F32 = jnp.float32
BF16 = jnp.bfloat16
MESH = pl.DeviceIdType.MESH


def nt(a, b):
    return lax.dot_general(a, b, (((1,), (1,)), ((), ())), preferred_element_type=F32)


def tn(a, b):
    return lax.dot_general(a, b, (((0,), (0,)), ((), ())), preferred_element_type=F32)


def mm(a, b):
    return jnp.dot(a, b, preferred_element_type=F32)


def split(a):
    high = a.astype(BF16)
    return high, (a - high.astype(F32)).astype(BF16)


def kernel(
    span_bits,
    head_axis,
    doc_ref,
    values_ref,
    gate_ref,
    key_ref,
    query_ref,
    step_ref,
    decay_ref,
    skip_ref,
    gain_ref,
    table_ref,
    pick_ref,
    out_ref,
    total_ref,
    factor_ref,
    score_ref,
    weighted_ref,
    gate_act_ref,
    sum_ref,
    block_ref,
    remote_ref,
    send_ref,
    recv_ref,
    decay_send_ref,
    decay_recv_ref,
    square_send_ref,
    square_recv_ref,
    send_sem,
    recv_sem,
    decay_send_sem,
    decay_recv_sem,
    square_send_sem,
    square_recv_sem,
):
    rows, width = values_ref.shape
    heads = step_ref.shape[1]
    states = key_ref.shape[1]
    stretches = rows // STRETCH
    low_bits = stretches.bit_length() - 1
    table_rows, _, level_count = table_ref.shape
    chunk = width // CHUNKS
    own_seq = lax.axis_index("seq")
    own_head = lax.axis_index("head")

    barrier = pltpu.get_barrier_semaphore()
    for bit in range(span_bits):
        pl.semaphore_signal(
            barrier,
            inc=1,
            device_id={"seq": own_seq ^ (1 << bit), "head": own_head},
            device_id_type=MESH,
        )
    for step in range(1, head_axis):
        pl.semaphore_signal(
            barrier,
            inc=1,
            device_id={"seq": own_seq, "head": lax.rem(own_head + step, head_axis)},
            device_id_type=MESH,
        )

    def state_copy(bit, j):
        return pltpu.make_async_remote_copy(
            src_ref=send_ref.at[bit, j],
            dst_ref=recv_ref.at[bit, j],
            send_sem=send_sem.at[bit, j],
            recv_sem=recv_sem.at[bit, j],
            device_id={"seq": own_seq ^ (1 << bit), "head": own_head},
            device_id_type=MESH,
        )

    def decay_copy(bit):
        return pltpu.make_async_remote_copy(
            src_ref=decay_send_ref.at[bit],
            dst_ref=decay_recv_ref.at[bit],
            send_sem=decay_send_sem.at[bit],
            recv_sem=decay_recv_sem.at[bit],
            device_id={"seq": own_seq ^ (1 << bit), "head": own_head},
            device_id_type=MESH,
        )

    def square_copy(step):
        return pltpu.make_async_remote_copy(
            src_ref=square_send_ref,
            dst_ref=square_recv_ref.at[step - 1],
            send_sem=square_send_sem.at[step - 1],
            recv_sem=square_recv_sem.at[step - 1],
            device_id={"seq": own_seq, "head": lax.rem(own_head + step, head_axis)},
            device_id_type=MESH,
        )

    row_id = lax.broadcasted_iota(jnp.int32, (rows, rows), 0)
    col_id = lax.broadcasted_iota(jnp.int32, (rows, rows), 1)
    lower = (row_id >= col_id).astype(F32).astype(BF16)
    log_decay = decay_ref[...]
    high, rest = split(log_decay)
    middle, low = split(log_decay - high.astype(F32))
    total = mm(lower, high) + (mm(lower, middle) + mm(lower, low))
    total_ref[...] = total
    end_log = total_ref[rows - 1 : rows, :]

    counts = []
    running = doc_ref[0]
    for c in range(stretches):
        if c:
            running = running + doc_ref[c]
        counts.append(running)

    def same(a, b):
        return (a == b).astype(F32)

    for c in range(stretches):
        here = slice(c * STRETCH, (c + 1) * STRETCH)
        factor_ref[0, here, :] = (
            jnp.exp(end_log - total_ref[here, :]) * step_ref[here, :] * same(counts[c], counts[-1])
        ).astype(BF16)

    head_row = lax.broadcasted_iota(jnp.int32, (heads, chunk), 0)
    head_lane = lax.broadcasted_iota(jnp.int32, (heads, chunk), 1) // HEADDIM

    def spread(j):
        return (head_row == head_lane + j * (chunk // HEADDIM)).astype(F32).astype(BF16)

    whole_row = lax.broadcasted_iota(jnp.int32, (heads, width), 0)
    whole_lane = lax.broadcasted_iota(jnp.int32, (heads, width), 1) // HEADDIM
    whole_spread = (whole_row == whole_lane).astype(F32).astype(BF16)

    def widen(row):
        a = jnp.broadcast_to(row, (16, heads))
        first, second = split(a)
        second, third = split(a - first.astype(F32))
        whole = mm(first, whole_spread) + (mm(second, whole_spread) + mm(third, whole_spread))
        return whole[0:1, :]

    span_decay = widen(jnp.exp(end_log)) * same(counts[-1], 0)
    decay_send_ref[0] = span_decay

    for j in range(CHUNKS):
        lanes = slice(j * chunk, (j + 1) * chunk)
        carried = (mm(factor_ref[0], spread(j)) * values_ref[:, lanes].astype(F32)).astype(BF16)
        state = tn(key_ref[...], carried)
        block_ref[j] = state
        send_ref[0, j] = state.astype(BF16)
        if j == 0:
            pl.semaphore_wait(barrier, span_bits + head_axis - 1)
            decay_copy(0).start()
        state_copy(0, j).start()

    part_row = lax.broadcasted_iota(jnp.int32, (table_rows * heads, level_count * heads), 0)
    part_lane = lax.broadcasted_iota(jnp.int32, (table_rows * heads, level_count * heads), 1)
    level_row = lax.broadcasted_iota(jnp.int32, (level_count, level_count * heads), 0)
    level_lane = lax.broadcasted_iota(jnp.int32, (level_count, level_count * heads), 1) // heads
    to_level = (level_row == level_lane).astype(F32).astype(BF16)
    table = table_ref[...].reshape(table_rows * heads, level_count)
    own = part_row % heads == part_lane % heads
    table_high, table_low = split(table)
    picked = (
        lax.broadcasted_iota(jnp.int32, (table_rows * heads, rows), 0) // heads == pick_ref[...]
    )
    picked = picked.astype(F32).astype(BF16)
    level_weight = tn(picked, jnp.where(own, mm(table_high, to_level), 0.0).astype(BF16)) + tn(
        picked, jnp.where(own, mm(table_low, to_level), 0.0).astype(BF16)
    )

    def weight(c, level):
        return level_weight[c * STRETCH : (c + 1) * STRETCH, level * heads : (level + 1) * heads]

    for c in range(stretches):
        here = slice(c * STRETCH, (c + 1) * STRETCH)
        log_here = total_ref[here, :]
        step_here = step_ref[here, :]
        middle_at = c * STRETCH + STRETCH // 2
        offset = log_here - total_ref[middle_at : middle_at + 1, :]
        factor_ref[1, here, :] = (jnp.exp(-offset) * step_here).astype(BF16)
        factor_ref[2, here, :] = (jnp.exp(offset) * weight(c, 0)).astype(BF16)
        for level in range(1, low_bits + 1):
            last = ((c >> level) << level) + (1 << (level - 1)) - 1
            edge = (last + 1) * STRETCH - 1
            keep = same(counts[c], counts[last])
            offset = log_here - total_ref[edge : edge + 1, :]
            if c >> (level - 1) & 1:
                value = jnp.exp(offset) * (weight(c, level) * keep)
            else:
                value = jnp.exp(-offset) * (step_here * keep)
            factor_ref[2 + level, here, :] = value.astype(BF16)
        reach = jnp.exp(log_here) * same(counts[c], 0)
        for bit in range(span_bits):
            upper = lax.rem(own_seq >> bit, 2).astype(F32)
            factor_ref[3 + low_bits + bit, here, :] = (
                reach * weight(c, 1 + low_bits + bit) * upper
            ).astype(BF16)

    tri_row = lax.broadcasted_iota(jnp.int32, (STRETCH, STRETCH), 0)
    tri_col = lax.broadcasted_iota(jnp.int32, (STRETCH, STRETCH), 1)
    for c in range(stretches):
        here = slice(c * STRETCH, (c + 1) * STRETCH)
        line = nt(query_ref[here, :], key_ref[0 : (c + 1) * STRETCH, :])
        if c:
            score_ref[here, 0 : c * STRETCH] = line[:, 0 : c * STRETCH].astype(BF16)
        score_ref[here, here] = jnp.where(tri_row >= tri_col, line[:, here], 0.0).astype(BF16)

    skip = widen(skip_ref[...])

    for j in range(CHUNKS):
        lanes = slice(j * chunk, (j + 1) * chunk)
        to_lanes = spread(j)
        values = values_ref[:, lanes].astype(F32)
        weighted_ref[...] = (mm(factor_ref[1], to_lanes) * values).astype(BF16)
        scale = mm(factor_ref[2], to_lanes)
        base = skip[:, lanes] * values
        for c in range(stretches):
            here = slice(c * STRETCH, (c + 1) * STRETCH)
            sum_ref[j, here, :] = base[here, :] + scale[here, :] * mm(
                score_ref[here, here], weighted_ref[here, :]
            )
        for level in range(1, low_bits + 1):
            half = STRETCH << (level - 1)
            scale = mm(factor_ref[2 + level], to_lanes)
            for start in range(0, rows, 2 * half):
                before = slice(start, start + half)
                after = slice(start + half, start + 2 * half)
                weighted = (scale[before, :] * values[before, :]).astype(BF16)
                sum_ref[j, after, :] += scale[after, :] * mm(score_ref[after, before], weighted)
        gate = gate_ref[:, lanes].astype(F32)
        gate_act_ref[j] = gate * (0.5 + 0.5 * jnp.tanh(0.5 * gate))

    def add_remote(bit, j):
        sum_ref[j] += mm(factor_ref[3 + low_bits + bit], spread(j)) * mm(
            query_ref[...], remote_ref[bit, j]
        )

    block_decay = span_decay
    lead_decay = jnp.ones_like(span_decay)
    for bit in range(span_bits):
        upper = lax.rem(own_seq >> bit, 2).astype(F32)
        decay_copy(bit).wait()
        other_decay = decay_recv_ref[bit]
        keep_own = upper + (1.0 - upper) * other_decay
        keep_other = upper * block_decay + (1.0 - upper)
        next_decay = block_decay * other_decay
        if bit + 1 < span_bits:
            decay_send_ref[bit + 1] = next_decay
            decay_copy(bit + 1).start()
        for j in range(CHUNKS):
            lanes = slice(j * chunk, (j + 1) * chunk)
            state_copy(bit, j).wait()
            other = recv_ref[bit, j].astype(F32)
            if bit + 1 < span_bits:
                merged = keep_own[:, lanes] * block_ref[j] + keep_other[:, lanes] * other
                block_ref[j] = merged
                send_ref[bit + 1, j] = merged.astype(BF16)
                state_copy(bit + 1, j).start()
            remote_ref[bit, j] = (lead_decay[:, lanes] * other).astype(BF16)
            if bit + 1 == span_bits:
                add_remote(bit, j)
        if bit + 1 < span_bits:
            for j in range(CHUNKS):
                add_remote(bit, j)
        lead_decay = lead_decay * (upper * other_decay + (1.0 - upper))
        block_decay = next_decay

    squares = jnp.zeros((rows, chunk), F32)
    for j in range(CHUNKS):
        gated = sum_ref[j] * gate_act_ref[j]
        sum_ref[j] = gated
        squares = squares + gated * gated
    ones = jnp.ones((16, chunk), BF16)
    square_high, square_low = split(squares)
    square_row = nt(ones, square_high) + nt(ones, square_low)
    square_send_ref[...] = square_row[0:1, :]
    for step in range(1, head_axis):
        square_copy(step).start()
    square_total = square_row[0:1, :]
    for step in range(1, head_axis):
        square_copy(step).wait()
        square_total = square_total + square_recv_ref[step - 1]
    mean_square = square_total * (1.0 / (width * head_axis))
    inverse = lax.rsqrt(mean_square + epsilon)
    inverse = jnp.broadcast_to(inverse, (8, rows)).T[:, 0:1]
    for j in range(CHUNKS):
        lanes = slice(j * chunk, (j + 1) * chunk)
        out_ref[:, lanes] = (sum_ref[j] * inverse * gain_ref[:, lanes]).astype(BF16)


def local(
    span_bits,
    head_axis,
    values_in,
    gate_in,
    key_proj,
    query_proj,
    step_size,
    log_decay,
    skip_weight,
    norm_gain,
    level_table,
    level_pick,
    doc_start,
):
    rows, width = values_in.shape
    heads = step_size.shape[1]
    states = key_proj.shape[1]
    low_bits = (rows // STRETCH).bit_length() - 1
    chunk = width // CHUNKS
    vmem = pl.BlockSpec(memory_space=pltpu.VMEM)
    bits = max(span_bits, 1)
    peers = max(head_axis - 1, 1)
    return pl.pallas_call(
        functools.partial(kernel, span_bits, head_axis),
        out_shape=jax.ShapeDtypeStruct((rows, width), BF16),
        in_specs=[pl.BlockSpec(memory_space=pltpu.SMEM)] + [vmem] * 10,
        out_specs=vmem,
        scratch_shapes=[
            pltpu.VMEM((rows, heads), F32),
            pltpu.VMEM((3 + low_bits + span_bits, rows, heads), BF16),
            pltpu.VMEM((rows, rows), BF16),
            pltpu.VMEM((rows, chunk), BF16),
            pltpu.VMEM((CHUNKS, rows, chunk), F32),
            pltpu.VMEM((CHUNKS, rows, chunk), F32),
            pltpu.VMEM((CHUNKS, states, chunk), F32),
            pltpu.VMEM((bits, CHUNKS, states, chunk), BF16),
            pltpu.VMEM((bits, CHUNKS, states, chunk), BF16),
            pltpu.VMEM((bits, CHUNKS, states, chunk), BF16),
            pltpu.VMEM((bits, 1, width), F32),
            pltpu.VMEM((bits, 1, width), F32),
            pltpu.VMEM((1, rows), F32),
            pltpu.VMEM((peers, 1, rows), F32),
            pltpu.SemaphoreType.DMA((bits, CHUNKS)),
            pltpu.SemaphoreType.DMA((bits, CHUNKS)),
            pltpu.SemaphoreType.DMA((bits,)),
            pltpu.SemaphoreType.DMA((bits,)),
            pltpu.SemaphoreType.DMA((peers,)),
            pltpu.SemaphoreType.DMA((peers,)),
        ],
        compiler_params=pltpu.CompilerParams(
            collective_id=0, has_side_effects=True, vmem_limit_bytes=48 * 1024 * 1024
        ),
    )(
        doc_start,
        values_in,
        gate_in,
        key_proj,
        query_proj,
        step_size,
        log_decay,
        skip_weight.reshape(1, heads),
        norm_gain.reshape(1, width),
        level_table,
        level_pick.reshape(1, rows),
    )


def solution(mesh):
    in_specs = (
        P("seq", "head"),
        P("seq", "head"),
        P("seq", None),
        P("seq", None),
        P("seq", "head"),
        P("seq", "head"),
        P("head"),
        P("head"),
        P(None, "head", None),
        P("seq"),
        P("seq"),
    )
    span_bits = mesh.shape["seq"].bit_length() - 1
    body = functools.partial(local, span_bits, mesh.shape["head"])
    return jax.shard_map(
        body, mesh=mesh, in_specs=in_specs, out_specs=P("seq", "head"), check_vma=False
    )
```

time: 108 us -> 39.6 us (0.37)
  waiting for transfers between devices: 37.9 us -> 0 us
  Pallas kernels: 0 us -> 33.1 us
  matrix products: 22.9 us -> 0 us
  other arithmetic: 16.8 us -> 0 us
  local copies, waits for them, and re-layouts: 15.1 us -> 6.1 us
  starting transfers between devices: 7.77 us -> 0 us
  blocking collectives: 5.66 us -> 0 us
    ppermute x5 -> x0, waiting for transfers between devices: 37.9 us -> none  [partner(): lax.ppermute(array, axis, [(i, i ^ 1 << distance) for i in range(lax.axis...]
    pallas_call x0 -> x1, Pallas kernels: none -> 33.1 us  [local(): pl.pallas_call(functools.partial(kernel, span_bits, head_axis), out_shape...]
    dot_general x11 -> x0, matrix products: 22.9 us -> none  [the longest x4 14.1 us: head_group(): jnp.einsum('hts,shp->thp', mixing, group_scaled.reshape(tok_rows, group_s...]
    ppermute x5 -> x0, starting transfers between devices: 7.77 us -> none  [partner(): lax.ppermute(array, axis, [(i, i ^ 1 << distance) for i in range(lax.axis...]
    psum x1 -> x0, blocking collectives: 5.66 us -> none  [local(): square_sum = lax.psum(jnp.sum(gated_out * gated_out, axis=1), 'head')]
    another operation x7 -> x0, other arithmetic: 5.55 us -> none
    eq x4 -> x0, other arithmetic: 3.76 us -> none  [head_group(): level_index[None] == level_id]
    dynamic_update_slice x4 -> x0, local copies, waits for them, and re-layouts: 3.39 us -> none  [local(): group_parts = lax.map(head_group, stacked)]
  transfers between devices with their start and end apart: 5 -> 0, of which waited for: 3 -> 0; matrix products, arithmetic and copies ran while one was open for 6% -> 0% of each run, Pallas kernels for 0% -> 0%
where the time goes in v1:
time: 39.6 us; the launch traced here: 39.3 us
  Pallas kernels  33.1 us (84%)
  local copies, waits for them, and re-layouts  6.1 us (15%)
    pallas_call x1, Pallas kernels, local(): pl.pallas_call(functools.partial(kernel, span_bits, head_axis), out_shape...  33.1 us
    unnamed x24, local copies, waits for them, and re-layouts  6.1 us

profile of v1, /device:TPU:0, one launch (start us, length us, event | category | flops | bytes accessed | tf_op | source)
XLA Modules:
  0.0 39.3 jit_solution(6663517239256823884)
XLA Ops:
  0.0 0.0 copy-start.8
  0.0 1.0 %copy.14.table_ref = f32[16,16,7]{2,1,0:T(8,128)S(1)} copy(f32[16,16,7]{1,0,2:T(8,128)} %param.19) | data formatting | bytes 14336 | tf_op args[8]
  1.0 0.0 copy-done.8
  1.0 0.0 copy-start.9
  1.0 0.1 copy.12.step_ref
  1.1 0.6 %copy-done.9 = f32[512,16]{0,1:T(8,128)S(1)} copy-done((f32[512,16]{0,1:T(8,128)S(1)}, f32[512,16]{0,1:T(8,128)}, u32[]{:S(2)}) %copy-start.9) | copy-done | bytes 32792
  1.8 0.0 copy-start.2
  1.8 0.0 copy-start.3
  1.8 0.0 copy-start.4
  1.8 0.0 copy-start.5
  1.8 0.0 copy-start.6
  1.8 0.0 copy-start.7
  1.8 0.1 copy.13.decay_ref
  1.9 0.7 %copy-done.2 = bf16[512,128]{1,0:T(8,128)(2,1)S(1)} copy-done((bf16[512,128]{1,0:T(8,128)(2,1)S(1)}, bf16[512,128]{1,0:T(8,128)(2,1)}, u32[]{:S(2)}) %copy-start.2) | copy-done | bytes 131096
  2.7 0.1 copy-done.3
  2.7 0.0 copy-done.4
  2.7 0.0 copy-done.5
  2.7 0.0 copy-done.6
  2.7 0.0 copy-done.7
  2.7 0.0 copy-start
  2.7 1.2 %copy-done = bf16[512,1024]{1,0:T(8,128)(2,1)S(1)} copy-done((bf16[512,1024]{1,0:T(8,128)(2,1)S(1)}, bf16[512,1024]{1,0:T(8,128)(2,1)}, u32[]{:S(2)}) %copy-start) | copy-done | bytes 1048600
  4.0 0.0 copy-start.1
  4.0 1.2 %copy-done.1 = bf16[512,1024]{1,0:T(8,128)(2,1)S(1)} copy-done((bf16[512,1024]{1,0:T(8,128)(2,1)S(1)}, bf16[512,1024]{1,0:T(8,128)(2,1)}, u32[]{:S(2)}) %copy-start.1) | copy-done | bytes 1048600
  5.2 33.1 %shard_map.109 = bf16[512,1024]{1,0:T(8,128)(2,1)S(1)} custom-call(s32[8]{0:T(128)S(1)} %copy-done.6, bf16[512,1024]{1,0:T(8,128)(2,1)S(1)} %copy-done, bf16[512,1024]{1,0:T(8,128)(2,1)S(1)} %copy-done.1, bf16[512,128]{1,0:T(8,128)(2,1)S(1)} %copy-done.2, bf16[512,128]{1,0:T(8,128)(2,1)S(1)} %copy-done.3, f32[512,16]{1,0:T(8,128)S(1)} %copy.12.step_ref, ...), custom_call_target="tpu_custom_call" | custom-call | tf_op jit(solution)/shard_map/pallas_call | solution.py:345
  38.3 1.0 %copy.16 = bf16[512,1024]{1,0:T(8,128)(2,1)} copy(bf16[512,1024]{1,0:T(8,128)(2,1)S(1)} %shard_map.109) | data formatting | bytes 2097152
Async XLA Ops:
  0.0 1.0 %copy-start.8 = (f32[512,16]{0,1:T(8,128)S(1)}, f32[512,16]{0,1:T(8,128)}, u32[]{:S(2)}) copy-start(f32[512,16]{0,1:T(8,128)} %param.15) | copy-start | bytes 98308
  1.0 0.8 %copy-start.9 = (f32[512,16]{0,1:T(8,128)S(1)}, f32[512,16]{0,1:T(8,128)}, u32[]{:S(2)}) copy-start(f32[512,16]{0,1:T(8,128)} %param.16) | copy-start | bytes 98308
  1.8 0.9 %copy-start.2 = (bf16[512,128]{1,0:T(8,128)(2,1)S(1)}, bf16[512,128]{1,0:T(8,128)(2,1)}, u32[]{:S(2)}) copy-start(bf16[512,128]{1,0:T(8,128)(2,1)} %key_ref.1) | copy-start | bytes 393220
  1.8 1.0 %copy-start.3 = (bf16[512,128]{1,0:T(8,128)(2,1)S(1)}, bf16[512,128]{1,0:T(8,128)(2,1)}, u32[]{:S(2)}) copy-start(bf16[512,128]{1,0:T(8,128)(2,1)} %query_ref.1) | copy-start | bytes 393220
  1.8 1.0 %copy-start.4 = (f32[1024]{0:T(1024)S(1)}, f32[1024]{0:T(1024)}, u32[]{:S(2)}) copy-start(f32[1024]{0:T(1024)} %param.18) | copy-start | bytes 12292
  1.8 1.0 %copy-start.5 = (s32[512]{0:T(512)S(1)}, s32[512]{0:T(512)}, u32[]{:S(2)}) copy-start(s32[512]{0:T(512)} %param.20) | copy-start | bytes 6148
  1.8 1.0 %copy-start.6 = (s32[8]{0:T(128)S(1)}, s32[8]{0:T(128)}, u32[]{:S(2)}) copy-start(s32[8]{0:T(128)} %doc_ref.1) | copy-start | bytes 100
  1.8 1.0 %copy-start.7 = (f32[16]{0:T(128)S(1)}, f32[16]{0:T(128)}, u32[]{:S(2)}) copy-start(f32[16]{0:T(128)} %param.17) | copy-start | bytes 196
  2.7 1.2 %copy-start = (bf16[512,1024]{1,0:T(8,128)(2,1)S(1)}, bf16[512,1024]{1,0:T(8,128)(2,1)}, u32[]{:S(2)}) copy-start(bf16[512,1024]{1,0:T(8,128)(2,1)} %values_ref.1) | copy-start | bytes 3145732
  4.0 1.2 %copy-start.1 = (bf16[512,1024]{1,0:T(8,128)(2,1)S(1)}, bf16[512,1024]{1,0:T(8,128)(2,1)}, u32[]{:S(2)}) copy-start(bf16[512,1024]{1,0:T(8,128)(2,1)} %gate_ref.1) | copy-start | bytes 3145732

commit v2 on v1

--- a/solution.py
+++ b/solution.py
@@ -37,7 +37,18 @@
 def kernel(
     span_bits,
     head_axis,
-    doc_ref,
+    values_hbm,
+    gate_hbm,
+    key_hbm,
+    query_hbm,
+    step_hbm,
+    decay_hbm,
+    skip_hbm,
+    gain_hbm,
+    table_hbm,
+    pick_hbm,
+    doc_hbm,
+    out_ref,
     values_ref,
     gate_ref,
     key_ref,
@@ -48,8 +59,9 @@
     gain_ref,
     table_ref,
     pick_ref,
-    out_ref,
-    total_ref,
+    doc_ref,
+    order_ref,
+    end_factor_ref,
     factor_ref,
     score_ref,
     weighted_ref,
@@ -63,6 +75,7 @@
     decay_recv_ref,
     square_send_ref,
     square_recv_ref,
+    load_sem,
     send_sem,
     recv_sem,
     decay_send_sem,
@@ -71,14 +84,34 @@
     square_recv_sem,
 ):
     rows, width = values_ref.shape
-    heads = step_ref.shape[1]
+    heads = step_ref.shape[0]
     states = key_ref.shape[1]
     stretches = rows // STRETCH
     low_bits = stretches.bit_length() - 1
-    table_rows, _, level_count = table_ref.shape
+    level_count, table_rows, _ = table_ref.shape
     chunk = width // CHUNKS
     own_seq = lax.axis_index("seq")
     own_head = lax.axis_index("head")
+
+    pairs = [
+        (decay_hbm, decay_ref),
+        (doc_hbm, doc_ref),
+        (step_hbm, step_ref),
+        (key_hbm, key_ref),
+        (values_hbm, values_ref),
+        (query_hbm, query_ref),
+        (pick_hbm, pick_ref),
+        (table_hbm, table_ref),
+        (skip_hbm, skip_ref),
+        (gain_hbm, gain_ref),
+        (gate_hbm, gate_ref),
+    ]
+    loads = [
+        pltpu.make_async_copy(source, target, load_sem.at[i])
+        for i, (source, target) in enumerate(pairs)
+    ]
+    for load in loads:
+        load.start()
 
     barrier = pltpu.get_barrier_semaphore()
     for bit in range(span_bits):
@@ -128,53 +161,70 @@
 
     row_id = lax.broadcasted_iota(jnp.int32, (rows, rows), 0)
     col_id = lax.broadcasted_iota(jnp.int32, (rows, rows), 1)
-    lower = (row_id >= col_id).astype(F32).astype(BF16)
+    order_ref[...] = (row_id <= col_id).astype(F32).astype(BF16)
+    whole_row = lax.broadcasted_iota(jnp.int32, (heads, width), 0)
+    whole_lane = lax.broadcasted_iota(jnp.int32, (heads, width), 1) // HEADDIM
+    whole_spread = (whole_row == whole_lane).astype(F32).astype(BF16)
+    lane = lax.broadcasted_iota(jnp.int32, (heads, rows), 1)
+
+    loads[0].wait()
+    loads[1].wait()
     log_decay = decay_ref[...]
     high, rest = split(log_decay)
     middle, low = split(log_decay - high.astype(F32))
-    total = mm(lower, high) + (mm(lower, middle) + mm(lower, low))
-    total_ref[...] = total
-    end_log = total_ref[rows - 1 : rows, :]
-
-    counts = []
-    running = doc_ref[0]
-    for c in range(stretches):
-        if c:
-            running = running + doc_ref[c]
-        counts.append(running)
-
-    def same(a, b):
-        return (a == b).astype(F32)
-
-    for c in range(stretches):
-        here = slice(c * STRETCH, (c + 1) * STRETCH)
-        factor_ref[0, here, :] = (
-            jnp.exp(end_log - total_ref[here, :]) * step_ref[here, :] * same(counts[c], counts[-1])
-        ).astype(BF16)
-
-    head_row = lax.broadcasted_iota(jnp.int32, (heads, chunk), 0)
-    head_lane = lax.broadcasted_iota(jnp.int32, (heads, chunk), 1) // HEADDIM
-
-    def spread(j):
-        return (head_row == head_lane + j * (chunk // HEADDIM)).astype(F32).astype(BF16)
-
-    whole_row = lax.broadcasted_iota(jnp.int32, (heads, width), 0)
-    whole_lane = lax.broadcasted_iota(jnp.int32, (heads, width), 1) // HEADDIM
-    whole_spread = (whole_row == whole_lane).astype(F32).astype(BF16)
-
-    def widen(row):
-        a = jnp.broadcast_to(row, (16, heads))
-        first, second = split(a)
-        second, third = split(a - first.astype(F32))
-        whole = mm(first, whole_spread) + (mm(second, whole_spread) + mm(third, whole_spread))
-        return whole[0:1, :]
-
-    span_decay = widen(jnp.exp(end_log)) * same(counts[-1], 0)
+    total = mm(jnp.concatenate([high, middle, low], axis=0), order_ref[...])
+    total = total[0:heads] + (total[heads : 2 * heads] + total[2 * heads : 3 * heads])
+    doc_row = lax.broadcasted_iota(jnp.int32, (stretches, rows), 0)
+    doc_lane = lax.broadcasted_iota(jnp.int32, (stretches, rows), 1) // STRETCH
+    doc_order = (doc_row <= doc_lane).astype(F32).astype(BF16)
+    doc = jnp.broadcast_to(doc_ref[...].astype(F32), (16, stretches)).astype(BF16)
+    count = mm(doc, doc_order)
+    if heads != 16:
+        count = jnp.broadcast_to(count[0:1], (heads, rows))
+
+    def at_edges(array, size, edge):
+        pieces = []
+        for start in range(0, rows, max(size, 128)):
+            piece = jnp.broadcast_to(
+                array[:, start + edge : start + edge + 1], (heads, max(size, 128))
+            )
+            if size < 128:
+                other = jnp.broadcast_to(
+                    array[:, start + size + edge : start + size + edge + 1], (heads, 128)
+                )
+                piece = jnp.where(lane[:, 0:128] < size, piece, other)
+            pieces.append(piece)
+        return jnp.concatenate(pieces, axis=1) if len(pieces) > 1 else pieces[0]
+
+    end_log = total[:, rows - 1 : rows]
+    end_count = count[:, rows - 1 : rows]
+    same_end = (count == end_count).astype(F32)
+    loads[2].wait()
+    step = step_ref[...]
+    end_factor = jnp.exp(end_log - total) * step * same_end
+    end_factor_ref[...] = end_factor.T.astype(BF16)
+
+    def widen(column):
+        a = jnp.broadcast_to(column, (heads, 128)).T[0:16, :]
+        first, rest = split(a)
+        second, third = split(rest32(a, first))
+        stacked = jnp.concatenate([first, second, third], axis=0)
+        whole = mm(stacked, whole_spread)
+        return whole[0:1] + (whole[16:17] + whole[32:33])
+
+    def rest32(a, first):
+        return a - first.astype(F32)
+
+    span_decay = widen(jnp.exp(end_log) * (end_count == 0.0).astype(F32))
     decay_send_ref[0] = span_decay
 
+    loads[3].wait()
+    loads[4].wait()
     for j in range(CHUNKS):
         lanes = slice(j * chunk, (j + 1) * chunk)
-        carried = (mm(factor_ref[0], spread(j)) * values_ref[:, lanes].astype(F32)).astype(BF16)
+        carried = (
+            mm(end_factor_ref[...], whole_spread[:, lanes]) * values_ref[:, lanes].astype(F32)
+        ).astype(BF16)
         state = tn(key_ref[...], carried)
         block_ref[j] = state
         send_ref[0, j] = state.astype(BF16)
@@ -183,49 +233,45 @@
             decay_copy(0).start()
         state_copy(0, j).start()
 
-    part_row = lax.broadcasted_iota(jnp.int32, (table_rows * heads, level_count * heads), 0)
-    part_lane = lax.broadcasted_iota(jnp.int32, (table_rows * heads, level_count * heads), 1)
-    level_row = lax.broadcasted_iota(jnp.int32, (level_count, level_count * heads), 0)
-    level_lane = lax.broadcasted_iota(jnp.int32, (level_count, level_count * heads), 1) // heads
-    to_level = (level_row == level_lane).astype(F32).astype(BF16)
-    table = table_ref[...].reshape(table_rows * heads, level_count)
-    own = part_row % heads == part_lane % heads
-    table_high, table_low = split(table)
+    for load in loads[5:]:
+        load.wait()
     picked = (
-        lax.broadcasted_iota(jnp.int32, (table_rows * heads, rows), 0) // heads == pick_ref[...]
+        lax.broadcasted_iota(jnp.int32, (table_rows, rows), 0) == pick_ref[...]
     )
     picked = picked.astype(F32).astype(BF16)
-    level_weight = tn(picked, jnp.where(own, mm(table_high, to_level), 0.0).astype(BF16)) + tn(
-        picked, jnp.where(own, mm(table_low, to_level), 0.0).astype(BF16)
-    )
-
-    def weight(c, level):
-        return level_weight[c * STRETCH : (c + 1) * STRETCH, level * heads : (level + 1) * heads]
-
-    for c in range(stretches):
-        here = slice(c * STRETCH, (c + 1) * STRETCH)
-        log_here = total_ref[here, :]
-        step_here = step_ref[here, :]
-        middle_at = c * STRETCH + STRETCH // 2
-        offset = log_here - total_ref[middle_at : middle_at + 1, :]
-        factor_ref[1, here, :] = (jnp.exp(-offset) * step_here).astype(BF16)
-        factor_ref[2, here, :] = (jnp.exp(offset) * weight(c, 0)).astype(BF16)
-        for level in range(1, low_bits + 1):
-            last = ((c >> level) << level) + (1 << (level - 1)) - 1
-            edge = (last + 1) * STRETCH - 1
-            keep = same(counts[c], counts[last])
-            offset = log_here - total_ref[edge : edge + 1, :]
-            if c >> (level - 1) & 1:
-                value = jnp.exp(offset) * (weight(c, level) * keep)
-            else:
-                value = jnp.exp(-offset) * (step_here * keep)
-            factor_ref[2 + level, here, :] = value.astype(BF16)
-        reach = jnp.exp(log_here) * same(counts[c], 0)
-        for bit in range(span_bits):
-            upper = lax.rem(own_seq >> bit, 2).astype(F32)
-            factor_ref[3 + low_bits + bit, here, :] = (
-                reach * weight(c, 1 + low_bits + bit) * upper
-            ).astype(BF16)
+
+    def weight(level):
+        table_high, table_low = split(table_ref[level])
+        return tn(table_high, picked) + tn(table_low, picked)
+
+    factors = []
+    offset = total - at_edges(total, STRETCH, STRETCH // 2)
+    factors.append(jnp.exp(-offset) * step)
+    factors.append(jnp.exp(offset) * weight(0))
+    for level in range(1, low_bits + 1):
+        size = STRETCH << level
+        offset = total - at_edges(total, size, size // 2 - 1)
+        keep = (count == at_edges(count, size, size // 2 - 1)).astype(F32)
+        after = lane % size >= size // 2
+        decayed = jnp.exp(jnp.minimum(jnp.where(after, offset, -offset), 0.0))
+        factors.append(decayed * keep * jnp.where(after, weight(level), step))
+    reach = jnp.exp(total) * (count == 0.0).astype(F32)
+    for bit in range(span_bits):
+        upper = lax.rem(own_seq >> bit, 2).astype(F32)
+        factors.append(reach * weight(1 + low_bits + bit) * upper)
+    per_group = 128 // heads
+    for group in range(factor_ref.shape[0]):
+        part = factors[group * per_group : (group + 1) * per_group]
+        part = part + [jnp.zeros((heads, rows), F32)] * (per_group - len(part))
+        factor_ref[group] = jnp.concatenate(part, axis=0).T.astype(BF16)
+
+    spread_row = lax.broadcasted_iota(jnp.int32, (128, chunk), 0)
+    spread_lane = lax.broadcasted_iota(jnp.int32, (128, chunk), 1) // HEADDIM
+
+    def spread(k, j):
+        first = (k % per_group) * heads + j * (chunk // HEADDIM)
+        pick = (spread_row == spread_lane + first).astype(F32).astype(BF16)
+        return mm(factor_ref[k // per_group], pick)
 
     tri_row = lax.broadcasted_iota(jnp.int32, (STRETCH, STRETCH), 0)
     tri_col = lax.broadcasted_iota(jnp.int32, (STRETCH, STRETCH), 1)
@@ -236,14 +282,16 @@
             score_ref[here, 0 : c * STRETCH] = line[:, 0 : c * STRETCH].astype(BF16)
         score_ref[here, here] = jnp.where(tri_row >= tri_col, line[:, here], 0.0).astype(BF16)
 
-    skip = widen(skip_ref[...])
-
-    for j in range(CHUNKS):
+    skip_high, skip_rest = split(jnp.broadcast_to(skip_ref[...], (16, heads)))
+    skip_low = (skip_ref[...] - skip_high[0:1].astype(F32)).astype(BF16)
+    skip = mm(skip_high, whole_spread) + mm(jnp.broadcast_to(skip_low, (16, heads)), whole_spread)
+    skip = skip[0:1, :]
+
+    def local_part(j):
         lanes = slice(j * chunk, (j + 1) * chunk)
-        to_lanes = spread(j)
         values = values_ref[:, lanes].astype(F32)
-        weighted_ref[...] = (mm(factor_ref[1], to_lanes) * values).astype(BF16)
-        scale = mm(factor_ref[2], to_lanes)
+        weighted_ref[...] = (spread(0, j) * values).astype(BF16)
+        scale = spread(1, j)
         base = skip[:, lanes] * values
         for c in range(stretches):
             here = slice(c * STRETCH, (c + 1) * STRETCH)
@@ -252,7 +300,7 @@
             )
         for level in range(1, low_bits + 1):
             half = STRETCH << (level - 1)
-            scale = mm(factor_ref[2 + level], to_lanes)
+            scale = spread(1 + level, j)
             for start in range(0, rows, 2 * half):
                 before = slice(start, start + half)
                 after = slice(start + half, start + 2 * half)
@@ -261,10 +309,11 @@
         gate = gate_ref[:, lanes].astype(F32)
         gate_act_ref[j] = gate * (0.5 + 0.5 * jnp.tanh(0.5 * gate))
 
+    for j in range(CHUNKS):
+        local_part(j)
+
     def add_remote(bit, j):
-        sum_ref[j] += mm(factor_ref[3 + low_bits + bit], spread(j)) * mm(
-            query_ref[...], remote_ref[bit, j]
-        )
+        sum_ref[j] += spread(2 + low_bits + bit, j) * mm(query_ref[...], remote_ref[bit, j])
 
     block_decay = span_decay
     lead_decay = jnp.ones_like(span_decay)
@@ -339,17 +388,34 @@
     states = key_proj.shape[1]
     low_bits = (rows // STRETCH).bit_length() - 1
     chunk = width // CHUNKS
-    vmem = pl.BlockSpec(memory_space=pltpu.VMEM)
+    hbm = pl.BlockSpec(memory_space=pltpu.HBM)
     bits = max(span_bits, 1)
     peers = max(head_axis - 1, 1)
+    factor_count = 2 + low_bits + span_bits
+    groups = -(-factor_count // (128 // heads))
+    operands = (
+        values_in,
+        gate_in,
+        key_proj,
+        query_proj,
+        step_size.T,
+        log_decay.T,
+        skip_weight.reshape(1, heads),
+        norm_gain.reshape(1, width),
+        level_table.transpose(2, 0, 1),
+        level_pick.reshape(1, rows),
+        doc_start.reshape(1, rows // STRETCH),
+    )
     return pl.pallas_call(
         functools.partial(kernel, span_bits, head_axis),
         out_shape=jax.ShapeDtypeStruct((rows, width), BF16),
-        in_specs=[pl.BlockSpec(memory_space=pltpu.SMEM)] + [vmem] * 10,
-        out_specs=vmem,
-        scratch_shapes=[
-            pltpu.VMEM((rows, heads), F32),
-            pltpu.VMEM((3 + low_bits + span_bits, rows, heads), BF16),
+        in_specs=[hbm] * len(operands),
+        out_specs=pl.BlockSpec(memory_space=pltpu.VMEM),
+        scratch_shapes=[pltpu.VMEM(a.shape, a.dtype) for a in operands]
+        + [
+            pltpu.VMEM((rows, rows), BF16),
+            pltpu.VMEM((rows, heads), BF16),
+            pltpu.VMEM((groups, rows, 128), BF16),
             pltpu.VMEM((rows, rows), BF16),
             pltpu.VMEM((rows, chunk), BF16),
             pltpu.VMEM((CHUNKS, rows, chunk), F32),
@@ -362,6 +428,7 @@
             pltpu.VMEM((bits, 1, width), F32),
             pltpu.VMEM((1, rows), F32),
             pltpu.VMEM((peers, 1, rows), F32),
+            pltpu.SemaphoreType.DMA((len(operands),)),
             pltpu.SemaphoreType.DMA((bits, CHUNKS)),
             pltpu.SemaphoreType.DMA((bits, CHUNKS)),
             pltpu.SemaphoreType.DMA((bits,)),
@@ -370,21 +437,9 @@
             pltpu.SemaphoreType.DMA((peers,)),
         ],
         compiler_params=pltpu.CompilerParams(
-            collective_id=0, has_side_effects=True, vmem_limit_bytes=48 * 1024 * 1024
+            collective_id=0, has_side_effects=True, vmem_limit_bytes=60 * 1024 * 1024
         ),
-    )(
-        doc_start,
-        values_in,
-        gate_in,
-        key_proj,
-        query_proj,
-        step_size,
-        log_decay,
-        skip_weight.reshape(1, heads),
-        norm_gain.reshape(1, width),
-        level_table,
-        level_pick.reshape(1, rows),
-    )
+    )(*operands)
 
 
 def solution(mesh):

time: 39.6 us -> 35.9 us (0.907)
  local copies, waits for them, and re-layouts: 6.1 us -> 2.26 us
  Pallas kernels: 33.1 us -> 33.5 us
    unnamed x24 -> x1, local copies, waits for them, and re-layouts: 6.1 us -> 2.26 us
where the time goes in v2:
time: 35.9 us; the launch traced here: 35.7 us
  Pallas kernels  33.5 us (93%)
  local copies, waits for them, and re-layouts  2.26 us (6%)
    pallas_call x1, Pallas kernels, local(): pl.pallas_call(functools.partial(kernel, span_bits, head_axis), out_shape...  33.5 us
    unnamed x1, local copies, waits for them, and re-layouts  2.26 us

profile of v2, /device:TPU:0, one launch (start us, length us, event | category | flops | bytes accessed | tf_op | source)
XLA Modules:
  0.0 35.7 jit_solution(14339284199672988927)
XLA Ops:
  0.0 33.5 %shard_map.109 = bf16[512,1024]{1,0:T(8,128)(2,1)} custom-call(bf16[512,1024]{1,0:T(8,128)(2,1)} %values_hbm.1, bf16[512,1024]{1,0:T(8,128)(2,1)} %gate_hbm.1, bf16[512,128]{1,0:T(8,128)(2,1)} %key_hbm.1, bf16[512,128]{1,0:T(8,128)(2,1)} %query_hbm.1, f32[16,512]{1,0:T(8,128)} %bitcast.8, f32[16,512]{1,0:T(8,128)} %bitcast.9, f32[1,16]{1,0:T(1,128)} %bitcast.12, ...), custom_call_target="tpu_custom_call" | custom-call | tf_op jit(solution)/shard_map/pallas_call | solution.py:409
  33.5 2.3 %copy.13 = bf16[512,1024]{1,0:T(8,128)(2,1)} copy(bf16[512,1024]{1,0:T(8,128)(2,1)} %shard_map.109) | data formatting | bytes 2097152

commit v3 on v2

--- a/solution.py
+++ b/solution.py
@@ -75,6 +75,8 @@
     decay_recv_ref,
     square_send_ref,
     square_recv_ref,
+    row_ref,
+    square_ref,
     load_sem,
     send_sem,
     recv_sem,
@@ -82,6 +84,7 @@
     decay_recv_sem,
     square_send_sem,
     square_recv_sem,
+    forward_sem,
 ):
     rows, width = values_ref.shape
     heads = step_ref.shape[0]
@@ -306,15 +309,42 @@
                 after = slice(start + half, start + 2 * half)
                 weighted = (scale[before, :] * values[before, :]).astype(BF16)
                 sum_ref[j, after, :] += scale[after, :] * mm(score_ref[after, before], weighted)
-        gate = gate_ref[:, lanes].astype(F32)
+
+    def gate_part(j):
+        gate = gate_ref[:, j * chunk : (j + 1) * chunk].astype(F32)
         gate_act_ref[j] = gate * (0.5 + 0.5 * jnp.tanh(0.5 * gate))
-
-    for j in range(CHUNKS):
-        local_part(j)
 
     def add_remote(bit, j):
         sum_ref[j] += spread(2 + low_bits + bit, j) * mm(query_ref[...], remote_ref[bit, j])
 
+    own_half = lax.rem(own_seq, 2)
+    last = span_bits - 1
+
+    def forward_copy(bit, i):
+        j = 2 * i + own_half
+        return pltpu.make_async_remote_copy(
+            src_ref=recv_ref.at[bit, j],
+            dst_ref=recv_ref.at[bit, j],
+            send_sem=forward_sem.at[bit, i],
+            recv_sem=recv_sem.at[bit, j],
+            device_id={"seq": own_seq ^ 1, "head": own_head},
+            device_id_type=MESH,
+        )
+
+    def merge(bit, j):
+        other = recv_ref[bit, j].astype(F32)
+        if bit < last:
+            merged = row_ref[0, j] * block_ref[j] + row_ref[1, j] * other
+            block_ref[j] = merged
+            send_ref[bit + 1, j] = merged.astype(BF16)
+        return other
+
+    def finish(j):
+        gated = sum_ref[j] * gate_act_ref[j]
+        sum_ref[j] = gated
+        square_ref[...] += gated * gated
+
+    square_ref[...] = jnp.zeros_like(square_ref)
     block_decay = span_decay
     lead_decay = jnp.ones_like(span_decay)
     for bit in range(span_bits):
@@ -324,32 +354,77 @@
         keep_own = upper + (1.0 - upper) * other_decay
         keep_other = upper * block_decay + (1.0 - upper)
         next_decay = block_decay * other_decay
-        if bit + 1 < span_bits:
+        if bit < last:
             decay_send_ref[bit + 1] = next_decay
             decay_copy(bit + 1).start()
         for j in range(CHUNKS):
             lanes = slice(j * chunk, (j + 1) * chunk)
-            state_copy(bit, j).wait()
-            other = recv_ref[bit, j].astype(F32)
-            if bit + 1 < span_bits:
-                merged = keep_own[:, lanes] * block_ref[j] + keep_other[:, lanes] * other
-                block_ref[j] = merged
-                send_ref[bit + 1, j] = merged.astype(BF16)
-                state_copy(bit + 1, j).start()
-            remote_ref[bit, j] = (lead_decay[:, lanes] * other).astype(BF16)
-            if bit + 1 == span_bits:
+            row_ref[0, j] = keep_own[:, lanes]
+            row_ref[1, j] = keep_other[:, lanes]
+            row_ref[2, j] = lead_decay[:, lanes]
+        if bit < 2:
+            for j in range(CHUNKS):
+                state_copy(bit, j).wait()
+                other = merge(bit, j)
+                if bit + 1 < min(2, span_bits):
+                    state_copy(bit + 1, j).start()
+                elif bit < last:
+
+                    @pl.when(own_half == j % 2)
+                    def _():
+                        state_copy(bit + 1, j).start()
+
+                remote_ref[bit, j] = (row_ref[2, j] * other).astype(BF16)
+                if bit == 0:
+                    local_part(j)
+                else:
+                    add_remote(0, j)
+            if bit == last:
+                for j in range(CHUNKS):
+                    add_remote(last, j)
+                    gate_part(j)
+            elif bit == 1:
+                for j in range(CHUNKS // 2):
+                    gate_part(j)
+        else:
+            for i in range(CHUNKS // 2):
+                j = 2 * i + own_half
+                state_copy(bit, j).wait()
+                forward_copy(bit, i).start()
+                if bit == 2:
+                    add_remote(1, 2 * i)
+                    add_remote(1, 2 * i + 1)
+                    gate_part(CHUNKS // 2 + i)
+            for i in range(CHUNKS // 2):
+                j = 2 * i + own_half
+                other = merge(bit, j)
+                if bit < last:
+                    state_copy(bit + 1, j).start()
+                remote_ref[bit, j] = (row_ref[2, j] * other).astype(BF16)
                 add_remote(bit, j)
-        if bit + 1 < span_bits:
-            for j in range(CHUNKS):
+                if bit == last:
+                    finish(j)
+            for i in range(CHUNKS // 2):
+                j = 2 * i + 1 - own_half
+                state_copy(bit, j).wait_recv()
+                other = merge(bit, j)
+                remote_ref[bit, j] = (row_ref[2, j] * other).astype(BF16)
                 add_remote(bit, j)
+                if bit == last:
+                    finish(j)
+            for i in range(CHUNKS // 2):
+                forward_copy(bit, i).wait_send()
         lead_decay = lead_decay * (upper * other_decay + (1.0 - upper))
         block_decay = next_decay
-
-    squares = jnp.zeros((rows, chunk), F32)
-    for j in range(CHUNKS):
-        gated = sum_ref[j] * gate_act_ref[j]
-        sum_ref[j] = gated
-        squares = squares + gated * gated
+    if span_bits == 0:
+        for j in range(CHUNKS):
+            local_part(j)
+            gate_part(j)
+    if span_bits < 3:
+        for j in range(CHUNKS):
+            finish(j)
+
+    squares = square_ref[...]
     ones = jnp.ones((16, chunk), BF16)
     square_high, square_low = split(squares)
     square_row = nt(ones, square_high) + nt(ones, square_low)
@@ -428,6 +503,8 @@
             pltpu.VMEM((bits, 1, width), F32),
             pltpu.VMEM((1, rows), F32),
             pltpu.VMEM((peers, 1, rows), F32),
+            pltpu.VMEM((3, CHUNKS, 1, chunk), F32),
+            pltpu.VMEM((rows, chunk), F32),
             pltpu.SemaphoreType.DMA((len(operands),)),
             pltpu.SemaphoreType.DMA((bits, CHUNKS)),
             pltpu.SemaphoreType.DMA((bits, CHUNKS)),
@@ -435,6 +512,7 @@
             pltpu.SemaphoreType.DMA((bits,)),
             pltpu.SemaphoreType.DMA((peers,)),
             pltpu.SemaphoreType.DMA((peers,)),
+            pltpu.SemaphoreType.DMA((bits, CHUNKS)),
         ],
         compiler_params=pltpu.CompilerParams(
             collective_id=0, has_side_effects=True, vmem_limit_bytes=60 * 1024 * 1024

time: 35.9 us -> 32.4 us (0.903)
  Pallas kernels: 33.5 us -> 30 us
    pallas_call x1, Pallas kernels: 33.5 us -> 30 us  [local(): pl.pallas_call(functools.partial(kernel, span_bits, head_axis), out_shape...]
where the time goes in v3:
time: 32.4 us; the launch traced here: 32.3 us
  Pallas kernels  30 us (93%)
  local copies, waits for them, and re-layouts  2.26 us (7%)
    pallas_call x1, Pallas kernels, local(): pl.pallas_call(functools.partial(kernel, span_bits, head_axis), out_shape...  30 us
    unnamed x1, local copies, waits for them, and re-layouts  2.26 us

profile of v3, /device:TPU:0, one launch (start us, length us, event | category | flops | bytes accessed | tf_op | source)
XLA Modules:
  0.0 32.3 jit_solution(2079864528081171314)
XLA Ops:
  0.0 30.0 %shard_map.109 = bf16[512,1024]{1,0:T(8,128)(2,1)} custom-call(bf16[512,1024]{1,0:T(8,128)(2,1)} %values_hbm.1, bf16[512,1024]{1,0:T(8,128)(2,1)} %gate_hbm.1, bf16[512,128]{1,0:T(8,128)(2,1)} %key_hbm.1, bf16[512,128]{1,0:T(8,128)(2,1)} %query_hbm.1, f32[16,512]{1,0:T(8,128)} %bitcast.8, f32[16,512]{1,0:T(8,128)} %bitcast.9, f32[1,16]{1,0:T(1,128)} %bitcast.12, ...), custom_call_target="tpu_custom_call" | custom-call | tf_op jit(solution)/shard_map/pallas_call | solution.py:484
  30.0 2.3 %copy.13 = bf16[512,1024]{1,0:T(8,128)(2,1)} copy(bf16[512,1024]{1,0:T(8,128)(2,1)} %shard_map.109) | data formatting | bytes 2097152
